TPU v7x, 32 devices: a whole 2x2x4 slice. The times are simulated.
32 devices in a mesh: bank: 4 (over z), zero: 8 (over y, x, core).
Axes of the slice: x: 2, y: 2, z: 4, core: 2. Of those that a mesh axis runs over, the one named last changes fastest.
Arguments:
- master_gate: float32 [64, 2048, 1024], P('bank', 'zero'), may hold values from -0.1875 to 0.1875
- second_gate: bfloat16 [64, 2048, 1024], P('bank', 'zero'), may hold values from -0.0625 to 0.0625
- master_up: float32 [64, 2048, 1024], P('bank', 'zero'), may hold values from -0.1875 to 0.1875
- second_up: bfloat16 [64, 2048, 1024], P('bank', 'zero'), may hold values from -0.0625 to 0.0625
- master_down: float32 [64, 1024, 2048], P('bank', None, 'zero'), may hold values from -0.25 to 0.25
- second_down: bfloat16 [64, 1024, 2048], P('bank', None, 'zero'), may hold values from -0.09375 to 0.09375
- router_weight: float32 [2048, 64], P('zero', 'bank'), may hold values from -0.125 to 0.125
- router_gain: float32 [2048], P('zero'), may hold values from 0.25 to 1.75
Outputs:
- final_gate: bfloat16 [64, 2048, 1024], P('bank', None, 'zero')
- final_up: bfloat16 [64, 2048, 1024], P('bank', None, 'zero')
- final_down: bfloat16 [64, 1024, 2048], P('bank', 'zero')
- scale_gate: float32 [64, 1024], P('bank', 'zero')
- scale_up: float32 [64, 1024], P('bank', 'zero')
- scale_down: float32 [64, 1024], P('bank', 'zero')
- serve_router: bfloat16 [2048, 64], replicated
All inputs are finite; a program needn't handle non-finite values. Where the computation divides by a largest or mean magnitude, that divisor is 1e-20 or more.
Results may differ from a plain program's by a relative error of at most 0.001.
Values may be sent and summed in bfloat16 or wider, within the bound.
A program may use at most 192 MiB of HBM per device.

v0:
```python
import jax
import jax.numpy as jnp
from jax import lax
from jax.experimental import pallas as pl
from jax.experimental.pallas import tpu as pltpu
from jax.sharding import PartitionSpec as P

f32, bf16 = jnp.float32, jnp.bfloat16


def cost(read_write, flops):
    return pl.CostEstimate(flops=flops, bytes_accessed=read_write, transcendentals=0)


def to_all(part, axes, count):
    same = jnp.broadcast_to(part[None], (count,) + part.shape)
    return lax.all_to_all(same, axes, split_axis=0, concat_axis=0, tiled=True)


def narrow_columns(master, second, inverse, zero):
    experts, rows, width = master.shape
    piece = width // zero
    step = 2 if experts % 2 == 0 else 1

    def body(master_ref, second_ref, inverse_ref, out_ref):
        for k in range(zero):
            cut = slice(k * piece, (k + 1) * piece)
            merged = master_ref[:, :, cut] + second_ref[:, :, cut].astype(f32)
            out_ref[k] = (merged * inverse_ref[:, :, cut]).astype(bf16)

    block = pl.BlockSpec((step, rows, width), lambda i: (i, 0, 0))
    return pl.pallas_call(
        body,
        grid=(experts // step,),
        in_specs=[block, block, pl.BlockSpec((step, 1, width), lambda i: (i, 0, 0))],
        out_specs=pl.BlockSpec((zero, step, rows, piece), lambda i: (0, i, 0, 0)),
        out_shape=jax.ShapeDtypeStruct((zero, experts, rows, piece), bf16),
        cost_estimate=cost(8 * master.size, 2 * master.size),
    )(master, second, inverse)


def join(pieces, axis):
    zero, experts, rows, columns = pieces.shape
    step = 2 if experts % 2 == 0 else 1
    shape = (zero * rows, columns) if axis == 1 else (rows, zero * columns)

    def body(in_ref, out_ref):
        for k in range(zero):
            if axis == 1:
                out_ref[:, k * rows : (k + 1) * rows, :] = in_ref[k]
            else:
                out_ref[:, :, k * columns : (k + 1) * columns] = in_ref[k]

    return pl.pallas_call(
        body,
        grid=(experts // step,),
        in_specs=[pl.BlockSpec((zero, step, rows, columns), lambda i: (0, i, 0, 0))],
        out_specs=pl.BlockSpec((step,) + shape, lambda i: (i, 0, 0)),
        out_shape=jax.ShapeDtypeStruct((experts,) + shape, pieces.dtype),
        cost_estimate=cost(4 * pieces.size, 0),
    )(pieces)


def exchange(pieces):
    return lax.all_to_all(pieces, "zero", split_axis=0, concat_axis=0, tiled=True)


def mine(scale, zero):
    width = scale.shape[1] // zero
    return lax.dynamic_slice_in_dim(scale, lax.axis_index("zero") * width, width, axis=1)


def aligned_device(sizes, mg, sg, mu, su, md, sd, router_weight, router_gain):
    bank, zero = sizes
    experts, rows, width = mg.shape
    model = rows * zero

    part_router = (router_weight * router_gain[:, None]).astype(bf16)
    router = to_all(part_router.reshape(-1, 128), ("bank", "zero"), bank * zero)

    part_up = jnp.sum(jnp.abs(mu + su.astype(f32)), axis=1)
    part_up, router = lax.optimization_barrier((part_up, router))
    all_up = to_all(part_up, "zero", zero)
    all_gate = to_all(jnp.sum(jnp.abs(mg + sg.astype(f32)), axis=1), "zero", zero)
    merged_down = md + sd.astype(f32)
    part_down = jnp.sum(jnp.abs(merged_down), axis=2)
    all_gate, all_up, part_down = lax.optimization_barrier((all_gate, all_up, part_down))
    all_down = to_all(part_down, "zero", zero)

    scale_gate = jnp.sum(all_gate, axis=0) / model
    narrow_gate = narrow_columns(mg, sg, (1.0 / scale_gate)[:, None, :], zero)
    narrow_gate, all_up, all_down = lax.optimization_barrier((narrow_gate, all_up, all_down))
    got_gate = exchange(narrow_gate)

    scale_up = jnp.sum(all_up, axis=0) / model
    narrow_up = narrow_columns(mu, su, (1.0 / scale_up)[:, None, :], zero)
    got_up = exchange(narrow_up)

    scale_down = jnp.sum(all_down, axis=0) / model
    narrow_down = (merged_down * (1.0 / scale_down)[:, :, None]).astype(bf16)
    split_down = narrow_down.reshape(experts, zero, width // zero, rows).transpose(1, 0, 2, 3)
    got_down = exchange(split_down)

    serve_router = (
        router.reshape(bank, zero, *part_router.shape).transpose(1, 2, 0, 3).reshape(model, -1)
    )
    return (
        join(got_gate, 1),
        join(got_up, 1),
        join(got_down, 2),
        mine(scale_gate, zero),
        mine(scale_up, zero),
        mine(scale_down, zero),
        serve_router,
    )


def general_device(sizes, mg, sg, mu, su, md, sd, router_weight, router_gain):
    zero = sizes[1]
    model = mg.shape[1] * zero
    merged = (mg + sg.astype(f32), mu + su.astype(f32), md + sd.astype(f32))
    totals = lax.psum(
        tuple(jnp.sum(jnp.abs(m), axis=a) for m, a in zip(merged, (1, 1, 2))), "zero"
    )
    scales = tuple(t / model for t in totals)
    finals = tuple(
        lax.all_to_all(
            (m / jnp.expand_dims(s, a)).astype(bf16),
            "zero", split_axis=3 - a, concat_axis=a, tiled=True,
        )
        for m, s, a in zip(merged, scales, (1, 1, 2))
    )
    part_router = (router_weight * router_gain[:, None]).astype(bf16)
    row_router = lax.all_gather(part_router, "zero", axis=0, tiled=True)
    serve_router = lax.all_gather(row_router, "bank", axis=1, tiled=True)
    return finals + tuple(mine(s, zero) for s in scales) + (serve_router,)


def solution(mesh):
    sizes = (mesh.shape["bank"], mesh.shape["zero"])

    def on_device(*args):
        _, rows, width = args[0].shape
        piece = width // sizes[1]
        tiles = piece % 128 == 0 and rows % 128 == 0 and args[6].size % 128 == 0
        return (aligned_device if tiles else general_device)(sizes, *args)

    return jax.shard_map(
        on_device,
        mesh=mesh,
        in_specs=(
            P("bank", "zero", None),
            P("bank", "zero", None),
            P("bank", "zero", None),
            P("bank", "zero", None),
            P("bank", None, "zero"),
            P("bank", None, "zero"),
            P("zero", "bank"),
            P("zero"),
        ),
        out_specs=(
            P("bank", None, "zero"),
            P("bank", None, "zero"),
            P("bank", "zero", None),
            P("bank", "zero"),
            P("bank", "zero"),
            P("bank", "zero"),
            P(),
        ),
        check_vma=False,
    )
```

profile of v0, /device:TPU:0, one launch (start us, length us, event | category | flops | bytes accessed | tf_op | source)
XLA Modules:
  0.0 373.5 jit_solution(12195049700325673007)
XLA Ops:
  0.6 0.7 multiply_convert_fusion.1
  1.6 0.7 broadcast_in_dim.12
  2.3 7.3 %all-to-all-start.1 = ((bf16[32,32,128]{2,1,0:T(8,128)(2,1)}), bf16[32,32,128]{2,1,0:T(8,128)(2,1)S(1)}, u32[]{:S(2)}, u32[]{:S(2)}) async-start(bf16[32,32,128]{2,1,0:T(8,128)(2,1)} %broadcast_in_dim.12), calls=%async_computation.1 | async-start | bytes 524288 | tf_op jit(solution)/shard_map/all_to_all | solution.py:17
  9.7 9.2 %abs_reduce_fusion.2 = f32[16,1024]{1,0:T(8,128)S(1)} fusion(f32[16,256,1024]{2,1,0:T(8,128)} %master_ref.2, bf16[16,256,1024]{2,1,0:T(8,128)(2,1)} %second_ref.2), kind=kLoop, calls=%fused_computation.4 | loop fusion | flops 16760832 | bytes 25231360 | tf_op jit(solution)/shard_map/reduce_sum | solution.py:84
  18.9 1.4 all-to-all-done.1
  20.2 0.8 broadcast_in_dim.10
  21.1 3.5 all-to-all-start
  24.6 9.2 %abs_reduce_fusion.1 = f32[16,1024]{1,0:T(8,128)S(1)} fusion(f32[16,256,1024]{2,1,0:T(8,128)} %master_ref.3, bf16[16,256,1024]{2,1,0:T(8,128)(2,1)} %second_ref.3), kind=kLoop, calls=%fused_computation.3 | loop fusion | flops 16760832 | bytes 25231360 | tf_op jit(solution)/shard_map/reduce_sum | solution.py:81
  34.2 0.8 broadcast_in_dim.13
  35.1 3.7 all-to-all-start.2
  38.8 9.1 %abs_reduce_fusion = f32[16,1024]{1,0:T(8,128)S(1)} fusion(f32[16,1024,256]{2,1,0:T(8,128)} %param.12, bf16[16,1024,256]{2,1,0:T(8,128)(2,1)} %param.13), kind=kLoop, calls=%fused_computation.1 | loop fusion | flops 16760832 | bytes 25231360 | tf_op jit(solution)/shard_map/reduce_sum | solution.py:86
  48.5 0.8 broadcast_in_dim.14
  49.3 3.6 all-to-all-start.3
  53.0 0.7 copy.20.inverse_ref
  53.7 13.5 %shard_map.135 = bf16[8,16,256,128]{3,2,1,0:T(8,128)(2,1)} custom-call(f32[16,256,1024]{2,1,0:T(8,128)} %master_ref.2, bf16[16,256,1024]{2,1,0:T(8,128)(2,1)} %second_ref.2, f32[16,1,1024]{2,1,0:T(1,128)} %copy.20.inverse_ref), custom_call_target="tpu_custom_call" | custom-call | flops 8388608 | bytes 33554432 | tf_op jit(solution)/shard_map/pallas_call | solution.py:32
  67.2 5.0 %all-to-all-start.4 = ((bf16[8,16,256,128]{3,2,1,0:T(8,128)(2,1)}), bf16[8,16,256,128]{3,2,1,0:T(8,128)(2,1)}, u32[]{:S(2)}, u32[]{:S(2)}) async-start(bf16[8,16,256,128]{3,2,1,0:T(8,128)(2,1)} %shard_map.135), calls=%async_computation.4 | async-start | bytes 16777216 | tf_op jit(solution)/shard_map/all_to_all | solution.py:65
  72.2 0.7 div.47.inverse_ref
  72.9 13.5 %shard_map.137 = bf16[8,16,256,128]{3,2,1,0:T(8,128)(2,1)} custom-call(f32[16,256,1024]{2,1,0:T(8,128)} %master_ref.3, bf16[16,256,1024]{2,1,0:T(8,128)(2,1)} %second_ref.3, f32[16,1,1024]{2,1,0:T(1,128)} %div.47.inverse_ref), custom_call_target="tpu_custom_call" | custom-call | flops 8388608 | bytes 33554432 | tf_op jit(solution)/shard_map/pallas_call | solution.py:32
  86.4 79.8 %all-to-all-done.4.in_ref = bf16[8,16,256,128]{3,2,1,0:T(8,128)(2,1)} async-done(((bf16[8,16,256,128]{3,2,1,0:T(8,128)(2,1)}), bf16[8,16,256,128]{3,2,1,0:T(8,128)(2,1)}, u32[]{:S(2)}, u32[]{:S(2)}) %all-to-all-start.4) | async-done | bytes 8388640 | tf_op jit(solution)/shard_map/all_to_all | solution.py:65
  166.2 5.0 %all-to-all-start.5 = ((bf16[8,16,256,128]{3,2,1,0:T(8,128)(2,1)}), bf16[8,16,256,128]{3,2,1,0:T(8,128)(2,1)}, u32[]{:S(2)}, u32[]{:S(2)}) async-start(bf16[8,16,256,128]{3,2,1,0:T(8,128)(2,1)} %shard_map.137), calls=%async_computation.5 | async-start | bytes 16777216 | tf_op jit(solution)/shard_map/all_to_all | solution.py:65
  171.3 12.0 %multiply_convert_fusion = bf16[16,1024,256]{2,1,0:T(8,128)(2,1)} fusion(f32[16,1024,256]{2,1,0:T(8,128)} %param.12, bf16[16,1024,256]{2,1,0:T(8,128)(2,1)} %param.13, f32[16,1024]{1,0:T(8,128)S(1)} %get-tuple-element.24), kind=kLoop, calls=%fused_computation | loop fusion | flops 16777216 | bytes 33619968 | tf_op jit(solution)/shard_map/convert_element_type | solution.py:100
  183.3 7.7 %copy.25 = bf16[16,8,128,256]{3,2,0,1:T(8,128)(2,1)} copy(bf16[16,8,128,256]{3,2,1,0:T(8,128)(2,1)} %bitcast.13) | data formatting | bytes 16777216 | tf_op jit(solution)/shard_map/reshape | solution.py:101
  191.0 74.3 %all-to-all-done.5.in_ref = bf16[8,16,256,128]{3,2,1,0:T(8,128)(2,1)} async-done(((bf16[8,16,256,128]{3,2,1,0:T(8,128)(2,1)}), bf16[8,16,256,128]{3,2,1,0:T(8,128)(2,1)}, u32[]{:S(2)}, u32[]{:S(2)}) %all-to-all-start.5) | async-done | bytes 8388640 | tf_op jit(solution)/shard_map/all_to_all | solution.py:65
  265.3 5.0 %all-to-all-start.6 = ((bf16[8,16,128,256]{3,2,1,0:T(8,128)(2,1)}), bf16[8,16,128,256]{3,2,1,0:T(8,128)(2,1)}, u32[]{:S(2)}, u32[]{:S(2)}) async-start(bf16[8,16,128,256]{3,2,1,0:T(8,128)(2,1)} %bitcast.12), calls=%async_computation.6 | async-start | bytes 16777216 | tf_op jit(solution)/shard_map/all_to_all | solution.py:65
  270.3 1.4 reshape.61
  271.6 0.9 copy.22
  272.5 0.8 copy.23
  273.9 0.6 constant_dynamic-slice_fusion
  274.5 9.0 %shard_map.136 = bf16[16,2048,128]{2,1,0:T(8,128)(2,1)} custom-call(bf16[8,16,256,128]{3,2,1,0:T(8,128)(2,1)} %all-to-all-done.4.in_ref), custom_call_target="tpu_custom_call" | custom-call | bytes 16777216 | tf_op jit(solution)/shard_map/pallas_call | solution.py:54
  283.4 9.0 %shard_map.138 = bf16[16,2048,128]{2,1,0:T(8,128)(2,1)} custom-call(bf16[8,16,256,128]{3,2,1,0:T(8,128)(2,1)} %all-to-all-done.5.in_ref), custom_call_target="tpu_custom_call" | custom-call | bytes 16777216 | tf_op jit(solution)/shard_map/pallas_call | solution.py:54
  292.4 71.9 %all-to-all-done.6.in_ref = bf16[8,16,128,256]{3,2,1,0:T(8,128)(2,1)} async-done(((bf16[8,16,128,256]{3,2,1,0:T(8,128)(2,1)}), bf16[8,16,128,256]{3,2,1,0:T(8,128)(2,1)}, u32[]{:S(2)}, u32[]{:S(2)}) %all-to-all-start.6) | async-done | bytes 8388640 | tf_op jit(solution)/shard_map/all_to_all | solution.py:65
  364.3 9.2 %shard_map.139 = bf16[16,128,2048]{2,1,0:T(8,128)(2,1)} custom-call(bf16[8,16,128,256]{3,2,1,0:T(8,128)(2,1)} %all-to-all-done.6.in_ref), custom_call_target="tpu_custom_call" | custom-call | bytes 16777216 | tf_op jit(solution)/shard_map/pallas_call | solution.py:54
  (12 shorter events, 2.0 us)
Async XLA Ops:
  2.3 17.9 %all-to-all-start.1 = ((bf16[32,32,128]{2,1,0:T(8,128)(2,1)}), bf16[32,32,128]{2,1,0:T(8,128)(2,1)S(1)}, u32[]{:S(2)}, u32[]{:S(2)}) async-start(bf16[32,32,128]{2,1,0:T(8,128)(2,1)} %broadcast_in_dim.12), calls=%async_computation.1 | async-start | bytes 524288 | tf_op jit(solution)/shard_map/all_to_all | solution.py:17
  21.1 13.2 %all-to-all-start = ((f32[8,16,1024]{2,1,0:T(8,128)}), f32[8,16,1024]{2,1,0:T(8,128)S(1)}, u32[]{:S(2)}, u32[]{:S(2)}) async-start(f32[8,16,1024]{2,1,0:T(8,128)} %broadcast_in_dim.10), calls=%async_computation | async-start | bytes 1048576 | tf_op jit(solution)/shard_map/all_to_all | solution.py:17
  35.1 13.4 %all-to-all-start.2 = ((f32[8,16,1024]{2,1,0:T(8,128)}), f32[8,16,1024]{2,1,0:T(8,128)S(1)}, u32[]{:S(2)}, u32[]{:S(2)}) async-start(f32[8,16,1024]{2,1,0:T(8,128)} %broadcast_in_dim.13), calls=%async_computation.2 | async-start | bytes 1048576 | tf_op jit(solution)/shard_map/all_to_all | solution.py:17
  49.3 17.9 %all-to-all-start.3 = ((f32[8,16,1024]{2,1,0:T(8,128)}), f32[8,16,1024]{2,1,0:T(8,128)S(1)}, u32[]{:S(2)}, u32[]{:S(2)}) async-start(f32[8,16,1024]{2,1,0:T(8,128)} %broadcast_in_dim.14), calls=%async_computation.3 | async-start | bytes 1048576 | tf_op jit(solution)/shard_map/all_to_all | solution.py:17
  67.2 99.0 %all-to-all-start.4 = ((bf16[8,16,256,128]{3,2,1,0:T(8,128)(2,1)}), bf16[8,16,256,128]{3,2,1,0:T(8,128)(2,1)}, u32[]{:S(2)}, u32[]{:S(2)}) async-start(bf16[8,16,256,128]{3,2,1,0:T(8,128)(2,1)} %shard_map.135), calls=%async_computation.4 | async-start | bytes 16777216 | tf_op jit(solution)/shard_map/all_to_all | solution.py:65
  166.2 99.1 %all-to-all-start.5 = ((bf16[8,16,256,128]{3,2,1,0:T(8,128)(2,1)}), bf16[8,16,256,128]{3,2,1,0:T(8,128)(2,1)}, u32[]{:S(2)}, u32[]{:S(2)}) async-start(bf16[8,16,256,128]{3,2,1,0:T(8,128)(2,1)} %shard_map.137), calls=%async_computation.5 | async-start | bytes 16777216 | tf_op jit(solution)/shard_map/all_to_all | solution.py:65
  265.3 99.0 %all-to-all-start.6 = ((bf16[8,16,128,256]{3,2,1,0:T(8,128)(2,1)}), bf16[8,16,128,256]{3,2,1,0:T(8,128)(2,1)}, u32[]{:S(2)}, u32[]{:S(2)}) async-start(bf16[8,16,128,256]{3,2,1,0:T(8,128)(2,1)} %bitcast.12), calls=%async_computation.6 | async-start | bytes 16777216 | tf_op jit(solution)/shard_map/all_to_all | solution.py:65
where the time goes:
time: 375 us; the launch traced here: 373 us
  waiting for transfers between devices  228 us (61%)
  Pallas kernels  54.1 us (14%)
  other arithmetic  40.3 us (11%)
  starting transfers between devices  33.1 us (9%)
  local copies, waits for them, and re-layouts  16.7 us (4%)
    all_to_all x3, waiting for transfers between devices, exchange(): lax.all_to_all(pieces, 'zero', split_axis=0, concat_axis=0, tiled=True)  226 us
    pallas_call x3, Pallas kernels, join(): pl.pallas_call(body, grid=(experts // step,), in_specs=[pl.BlockSpec((zer...  27.1 us
    pallas_call x2, Pallas kernels, narrow_columns(): pl.pallas_call(body, grid=(experts // step,), in_specs=[block, block, pl....  27 us
    all_to_all x4, starting transfers between devices, to_all(): return lax.all_to_all(same, axes, split_axis=0, concat_axis=0, tiled=True)  18.1 us
    all_to_all x3, starting transfers between devices, exchange(): lax.all_to_all(pieces, 'zero', split_axis=0, concat_axis=0, tiled=True)  15 us
    convert_element_type x1, other arithmetic, aligned_device(): narrow_down = (merged_down * (1.0 / scale_down)[:, :, None]).astype(bf16)  12 us
    reduce_sum x1, other arithmetic, aligned_device(): jnp.sum(jnp.abs(mg + sg.astype(f32)), axis=1)  9.19 us
    reduce_sum x1, other arithmetic, aligned_device(): part_up = jnp.sum(jnp.abs(mu + su.astype(f32)), axis=1)  9.19 us
  transfers between devices with their start and end apart: 7, of which 6 were waited for; matrix products, arithmetic and copies ran while one was open for 14% of the time, Pallas kernels for 12%

commit v1 on v0

v1 whole, which is shorter than its diff:
```python
import functools

import jax
import jax.numpy as jnp
from jax import lax
from jax.experimental import pallas as pl
from jax.experimental.pallas import tpu as pltpu
from jax.sharding import PartitionSpec as P

f32, bf16 = jnp.float32, jnp.bfloat16
MESH = pl.DeviceIdType.MESH
GROUP = 8
FIRST = 2
AHEAD = 4
READS = 2
SLOTS = 4


def flip(index, bits, size):
    out, bit = 0, 1
    while bit < size:
        own = (index // bit) % 2
        out = out + bit * ((1 - own) if bits & bit else own)
        bit *= 2
    return out


def send_order(zero):
    return sorted(range(1, zero), key=lambda d: (d == 1, d & 1, -d))


def exchange_kernel(bank, zero, *refs):
    (mg, sg, mu, su, md, sd, rw, gain,
     land_gate, land_up, land_down, scale_gate, scale_up, scale_down, router,
     sum_m, sum_s, sum_dm, sum_ds, in_m, in_s, in_dm, in_ds, stage, stage_down,
     first, first_got, first_inv, part, part_got, total, inverse,
     rw_v, gain_v, router_part,
     sum_sem, in_sem, stage_sem, data_sem, small_sem, router_sem) = refs
    experts, rows, width = mg.shape
    piece = width // zero
    model = rows * zero
    per = experts // GROUP
    me = lax.axis_index("zero")
    my_bank = lax.axis_index("bank")
    masters, seconds = (mg, mu, md), (sg, su, sd)
    lands = (land_gate, land_up, land_down)
    scales = (scale_gate, scale_up, scale_down)
    order = send_order(zero)

    def peer(d):
        return flip(me, d, zero)

    def columns(k):
        return pl.ds(pl.multiple_of(k * piece, piece), piece)

    def send(src, dst, send_sem, recv_sem, d):
        pltpu.make_async_remote_copy(
            src_ref=src, dst_ref=dst, send_sem=send_sem, recv_sem=recv_sem,
            device_id={"zero": peer(d)}, device_id_type=MESH,
        ).start()

    def await_bytes(ref, sem):
        pltpu.make_async_copy(ref, ref, sem).wait()

    def reads(m, e, slot, bufs, sem):
        return (
            pltpu.make_async_copy(masters[m].at[e], bufs[0].at[slot], sem.at[0, slot]),
            pltpu.make_async_copy(seconds[m].at[e], bufs[1].at[slot], sem.at[1, slot]),
        )

    def sum_reads(m, e, slot):
        bufs = (sum_m, sum_s) if m < 2 else (sum_dm, sum_ds)
        return reads(m, e, slot, bufs, sum_sem.at[int(m == 2)])

    def scale_reads(m, e, slot):
        bufs = (in_m, in_s) if m < 2 else (in_dm, in_ds)
        return reads(m, e, slot, bufs, in_sem.at[int(m == 2)])

    def start(copies):
        for c in copies:
            c.start()

    def finish(copies):
        for c in copies:
            c.wait()


    def row_sum(m_ref, s_ref):
        def body(i, acc):
            r = pl.ds(pl.multiple_of(i * 16, 16), 16)
            x = jnp.abs(m_ref[r, :] + s_ref[r, :].astype(f32))
            return acc + (x[:8] + x[8:])

        acc = lax.fori_loop(0, rows // 16, body, jnp.zeros((8, width), f32), unroll=4)
        return jnp.sum(acc, axis=0, keepdims=True)

    def store_column_sums(m_ref, s_ref, g, j):
        found = []
        for k in range(width // 128):
            r = slice(k * 128, (k + 1) * 128)
            acc = None
            for c in range(rows // 128):
                cut = slice(c * 128, (c + 1) * 128)
                x = jnp.abs(m_ref[r, cut] + s_ref[r, cut].astype(f32))
                acc = x if acc is None else acc + x
            found.append(jnp.sum(acc.T, axis=0, keepdims=True))
        part[g, pl.ds(j, 1), :] = jnp.concatenate(found, axis=1)

    def sum_experts(g, low, high, last=True):
        m, base = g // per, (g % per) * GROUP

        def body(j, _):
            slot = lax.rem(j, AHEAD)
            finish(sum_reads(m, base + j, slot))
            if m < 2:
                v = row_sum(sum_m.at[slot], sum_s.at[slot])
                part[g, pl.ds(j, 1), :] = v
                if high == FIRST:
                    first[pl.ds(j, 1), :] = v
            else:
                store_column_sums(sum_dm.at[slot], sum_ds.at[slot], g, j)

            @pl.when(j + AHEAD < GROUP)
            def _():
                start(sum_reads(m, base + j + AHEAD, slot))

            return 0

        lax.fori_loop(low, high, body, 0)
        if last and g + 1 < 3 * per:
            for j in range(AHEAD):
                start(sum_reads((g + 1) // per, ((g + 1) % per) * GROUP + j, j))

    def scatter_sums(g):
        for d in order:
            send(part.at[g, :, columns(peer(d))], part_got.at[g, d - 1],
                 small_sem.at[0, g], small_sem.at[1, g], d)

    def gather_totals(g):
        await_bytes(part_got.at[g], small_sem.at[1, g])
        t = part[g, :, columns(me)]
        for d in range(1, zero):
            t = t + part_got[g, d - 1]
        total[g, :, columns(me)] = t
        m, base = g // per, (g % per) * GROUP
        scales[m][base : base + GROUP, :] = t / model
        for d in order:
            mine = total.at[g, :, columns(me)]
            send(mine, mine, small_sem.at[2, g], small_sem.at[3, g], d)

    def take_totals(g):
        await_bytes(part_got.at[g], small_sem.at[3, g])
        for k in range(zero):
            inverse[g, k] = 1.0 / (total[g, :, k * piece : (k + 1) * piece] / model)


    def send_expert(m, e, row, slot, fresh=False):
        finish(scale_reads(m, e, lax.rem(e, READS)))
        b = lax.rem(e, READS)
        staged = stage if m < 2 else stage_down
        sem = stage_sem.at[int(m == 2), slot]
        if not fresh:
            await_bytes(staged.at[slot], sem)
        half = rows // 2
        for d in order + [0]:
            k = peer(d)
            cut = columns(k)
            scale = row(k)
            if m < 2:
                for h in range(2):
                    r = slice(h * half, (h + 1) * half)
                    x = (in_m[b, r, cut] + in_s[b, r, cut].astype(f32)) * scale
                    if d:
                        stage[slot, d - 1, r, :] = x.astype(bf16)
                    else:
                        at = pl.ds(pl.multiple_of(me * rows + h * half, half), half)
                        lands[m][e, at, :] = x.astype(bf16)
                there = lands[m].at[e, pl.ds(pl.multiple_of(me * rows, rows), rows)]
            else:
                t = jnp.broadcast_to(scale, (128, piece)).T
                for c in range(rows // 128):
                    r = slice(c * 128, (c + 1) * 128)
                    x = (in_dm[b, cut, r] + in_ds[b, cut, r].astype(f32)) * t
                    if d:
                        stage_down[slot, d - 1, :, r] = x.astype(bf16)
                    else:
                        land_down[e, me, :, r] = x.astype(bf16)
                there = land_down.at[e, me]
            if d:
                send(staged.at[slot, d - 1], there, sem, data_sem.at[m, d - 1], d)

    def scaled_row(g, j):
        return lambda k: inverse[g, k, pl.ds(j, 1), :]

    def send_range(m, low, high, fresh=False):
        def body(e, _):
            send_expert(m, e, scaled_row(m * per + e // GROUP, lax.rem(e, GROUP)),
                        lax.rem(e, SLOTS), fresh)

            @pl.when(e + READS < experts)
            def _():
                start(scale_reads(m, e + READS, lax.rem(e, READS)))

            return 0

        lax.fori_loop(low, high, body, 0)


    c = rw.shape[0]
    own_experts = pl.ds(pl.multiple_of(my_bank * c, c), c)
    own_rows = pl.ds(pl.multiple_of(me * rows, rows), rows)

    def router_reads():
        return (
            pltpu.make_async_copy(rw, rw_v, router_sem.at[0]),
            pltpu.make_async_copy(gain, gain_v, router_sem.at[1]),
        )

    def send_router():
        finish(router_reads())
        router_part[...] = (rw_v[...] * gain_v[...]).astype(bf16)
        router[own_experts, own_rows] = router_part[...]
        for d in order:
            send(router_part, router.at[own_experts, own_rows], router_sem.at[2], router_sem.at[3], d)

    def share_router():
        await_bytes(router.at[pl.ds(0, c), pl.ds(0, (zero - 1) * rows)], router_sem.at[3])
        for d in range(1, bank):
            pltpu.make_async_remote_copy(
                src_ref=router.at[own_experts], dst_ref=router.at[own_experts],
                send_sem=router_sem.at[4], recv_sem=router_sem.at[5],
                device_id={"bank": (my_bank + d) % bank}, device_id_type=MESH,
            ).start()


    barrier = pltpu.get_barrier_semaphore()
    for d in range(1, zero):
        pl.semaphore_signal(barrier, inc=1, device_id={"zero": peer(d)}, device_id_type=MESH)
    for d in range(1, bank):
        pl.semaphore_signal(
            barrier, inc=1, device_id={"bank": (my_bank + d) % bank}, device_id_type=MESH)

    for j in range(AHEAD):
        start(sum_reads(0, j, j))
    for j in range(READS):
        start(scale_reads(0, j, j))
        start(scale_reads(2, j, j))
    start(router_reads())
    sum_experts(0, 0, FIRST, last=False)
    pl.semaphore_wait(barrier, zero - 1 + bank - 1)
    for d in order:
        send(first, first_got.at[d - 1], small_sem.at[4, 0], small_sem.at[4, 1], d)
    sum_experts(0, FIRST, GROUP)
    scatter_sums(0)
    await_bytes(first_got, small_sem.at[4, 1])
    t = first[...]
    for d in range(1, zero):
        t = t + first_got[d - 1]
    for k in range(zero):
        first_inv[k] = 1.0 / (t[:, k * piece : (k + 1) * piece] / model)

    def send_first(j):
        send_expert(0, j, lambda k: first_inv[k, j : j + 1, :], j, fresh=True)
        start(scale_reads(0, j + READS, j % READS))

    send_first(0)
    sum_experts(1, 0, GROUP)
    scatter_sums(1)
    gather_totals(0)
    send_first(1)
    send_router()
    take_totals(0)
    send_range(0, 2, 4, fresh=True)
    gather_totals(1)
    sum_experts(2, 0, GROUP)
    scatter_sums(2)
    send_range(0, 4, 6)
    sum_experts(3, 0, GROUP)
    scatter_sums(3)
    send_range(0, 6, 7)
    gather_totals(2)
    send_range(0, 7, 8)
    take_totals(1)
    send_range(0, 8, 10)
    sum_experts(4, 0, GROUP)
    scatter_sums(4)
    gather_totals(3)
    send_range(0, 10, 12)
    sum_experts(5, 0, GROUP)
    scatter_sums(5)
    share_router()
    send_range(0, 12, 14)
    gather_totals(4)
    send_range(0, 14, 16)
    for j in range(READS):
        start(scale_reads(1, j, j))
    gather_totals(5)
    take_totals(2)
    take_totals(3)
    send_range(1, 0, 4)
    take_totals(4)
    take_totals(5)
    send_range(1, 4, 16)
    send_range(2, 0, SLOTS, fresh=True)
    send_range(2, SLOTS, experts)

    for s in range(SLOTS):
        await_bytes(stage.at[s], stage_sem.at[0, s])
        await_bytes(stage_down.at[s], stage_sem.at[1, s])
    await_bytes(first_got, small_sem.at[4, 0])
    for g in range(3 * per):
        await_bytes(part_got.at[g], small_sem.at[0, g])
        await_bytes(part_got.at[g], small_sem.at[2, g])
    await_bytes(router.at[pl.ds(0, c), pl.ds(0, (zero - 1) * rows)], router_sem.at[2])
    if bank > 1:
        await_bytes(router.at[pl.ds(0, (bank - 1) * c)], router_sem.at[4])
        await_bytes(router.at[pl.ds(0, (bank - 1) * c)], router_sem.at[5])
    for d in range(1, zero):
        await_bytes(land_gate.at[:, pl.ds(0, rows)], data_sem.at[0, d - 1])
        await_bytes(land_up.at[:, pl.ds(0, rows)], data_sem.at[1, d - 1])
        await_bytes(land_down.at[:, 0], data_sem.at[2, d - 1])


def store_kernel(zero, *refs):
    gate, up, down, *small = refs[:7]
    out_gate, out_up, out_down, *small_out = refs[7:14]
    sem = refs[14]
    rows = down.shape[3]
    copies = []
    for src, dst in ((gate, out_gate), (up, out_up)):
        for k in range(zero):
            at = pl.ds(k * (src.shape[0] // zero), src.shape[0] // zero)
            copies.append((src.at[at], dst.at[at]))
    for k in range(zero):
        copies.append((down.at[:, k], out_down.at[:, :, k * rows : (k + 1) * rows]))
    copies += list(zip(small, small_out))
    copies = [pltpu.make_async_copy(s, d, sem.at[i]) for i, (s, d) in enumerate(copies)]
    for c in copies:
        c.start()
    for c in copies:
        c.wait()


def fast_device(sizes, mg, sg, mu, su, md, sd, router_weight, router_gain):
    bank, zero = sizes
    experts, rows, width = mg.shape
    piece = width // zero
    c = router_weight.shape[1]
    groups = 3 * experts // GROUP
    anywhere = pl.BlockSpec(memory_space=pl.ANY)
    vmem = pl.BlockSpec(memory_space=pltpu.VMEM)
    shapes = (
        ((experts, zero * rows, piece), bf16),
        ((experts, zero * rows, piece), bf16),
        ((experts, zero, piece, rows), bf16),
        ((experts, piece), f32),
        ((experts, piece), f32),
        ((experts, piece), f32),
        ((bank * c, zero * rows), bf16),
    )
    dma = pltpu.SemaphoreType.DMA
    landed = pl.pallas_call(
        functools.partial(exchange_kernel, bank, zero),
        in_specs=[anywhere] * 8,
        out_specs=[vmem] * 7,
        out_shape=[pltpu.VMEM(*s) for s in shapes],
        scratch_shapes=[
            pltpu.VMEM((AHEAD, rows, width), f32),
            pltpu.VMEM((AHEAD, rows, width), bf16),
            pltpu.VMEM((AHEAD, width, rows), f32),
            pltpu.VMEM((AHEAD, width, rows), bf16),
            pltpu.VMEM((READS, rows, width), f32),
            pltpu.VMEM((READS, rows, width), bf16),
            pltpu.VMEM((READS, width, rows), f32),
            pltpu.VMEM((READS, width, rows), bf16),
            pltpu.VMEM((SLOTS, zero - 1, rows, piece), bf16),
            pltpu.VMEM((SLOTS, zero - 1, piece, rows), bf16),
            pltpu.VMEM((FIRST, width), f32),
            pltpu.VMEM((zero - 1, FIRST, width), f32),
            pltpu.VMEM((zero, FIRST, piece), f32),
            pltpu.VMEM((groups, GROUP, width), f32),
            pltpu.VMEM((groups, zero - 1, GROUP, piece), f32),
            pltpu.VMEM((groups, GROUP, width), f32),
            pltpu.VMEM((groups, zero, GROUP, piece), f32),
            pltpu.VMEM((c, rows), f32),
            pltpu.VMEM((1, rows), f32),
            pltpu.VMEM((c, rows), bf16),
            dma((2, 2, AHEAD)),
            dma((2, 2, READS)),
            dma((2, SLOTS)),
            dma((3, zero - 1)),
            dma((5, groups)),
            dma((6,)),
        ],
        compiler_params=pltpu.CompilerParams(
            collective_id=0, has_side_effects=True, vmem_limit_bytes=34 << 20),
    )(mg, sg, mu, su, md, sd, router_weight.T, router_gain.reshape(1, -1))
    outs = shapes[:2] + (((experts, piece, zero * rows), bf16),) + shapes[3:]
    *stored, router = pl.pallas_call(
        functools.partial(store_kernel, zero),
        in_specs=[vmem] * 7,
        out_specs=[anywhere] * 7,
        out_shape=[jax.ShapeDtypeStruct(*s) for s in outs],
        scratch_shapes=[dma((3 * zero + 4,))],
        compiler_params=pltpu.CompilerParams(vmem_limit_bytes=1 << 20),
    )(*landed)
    return (*stored, router.T)


def mine(scale, zero):
    width = scale.shape[1] // zero
    return lax.dynamic_slice_in_dim(scale, lax.axis_index("zero") * width, width, axis=1)


def general_device(sizes, mg, sg, mu, su, md, sd, router_weight, router_gain):
    zero = sizes[1]
    model = mg.shape[1] * zero
    merged = (mg + sg.astype(f32), mu + su.astype(f32), md + sd.astype(f32))
    totals = lax.psum(
        tuple(jnp.sum(jnp.abs(m), axis=a) for m, a in zip(merged, (1, 1, 2))), "zero"
    )
    scales = tuple(t / model for t in totals)
    finals = tuple(
        lax.all_to_all(
            (m / jnp.expand_dims(s, a)).astype(bf16),
            "zero", split_axis=3 - a, concat_axis=a, tiled=True,
        )
        for m, s, a in zip(merged, scales, (1, 1, 2))
    )
    part_router = (router_weight * router_gain[:, None]).astype(bf16)
    row_router = lax.all_gather(part_router, "zero", axis=0, tiled=True)
    serve_router = lax.all_gather(row_router, "bank", axis=1, tiled=True)
    return finals + tuple(mine(s, zero) for s in scales) + (serve_router,)


def fits(sizes, mg, router_weight):
    zero = sizes[1]
    experts, rows, width = mg.shape
    c = router_weight.shape[1]
    if zero < 2 or zero & (zero - 1) or experts != 2 * GROUP or experts % zero:
        return False
    if width % zero or (width // zero) % 128 or rows % 256 or c % 16:
        return False
    unit = rows * width
    held = 3 * experts * unit * 2 + 2 * (6 * (AHEAD + READS) + 2 * SLOTS) * unit
    return held <= 52 << 20


def solution(mesh):
    sizes = (mesh.shape["bank"], mesh.shape["zero"])

    def on_device(*args):
        fast = fits(sizes, args[0], args[6])
        return (fast_device if fast else general_device)(sizes, *args)

    return jax.shard_map(
        on_device,
        mesh=mesh,
        in_specs=(
            P("bank", "zero", None),
            P("bank", "zero", None),
            P("bank", "zero", None),
            P("bank", "zero", None),
            P("bank", None, "zero"),
            P("bank", None, "zero"),
            P("zero", "bank"),
            P("zero"),
        ),
        out_specs=(
            P("bank", None, "zero"),
            P("bank", None, "zero"),
            P("bank", "zero", None),
            P("bank", "zero"),
            P("bank", "zero"),
            P("bank", "zero"),
            P(),
        ),
        check_vma=False,
    )
```

time: 375 us -> 296 us (0.79)
  Pallas kernels: 54.1 us -> 295 us
  waiting for transfers between devices: 228 us -> 0 us
  other arithmetic: 40.3 us -> 0 us
  starting transfers between devices: 33.1 us -> 0 us
  local copies, waits for them, and re-layouts: 16.7 us -> 0 us
    pallas_call x5 -> x2, Pallas kernels: 54.1 us -> 295 us  [the longest x1 287 us: fast_device(): pl.pallas_call(functools.partial(exchange_kernel, bank, zero), in_specs=[...]
    all_to_all x7 -> x0, waiting for transfers between devices: 228 us -> none  [the longest x3 226 us: exchange(): lax.all_to_all(pieces, 'zero', split_axis=0, concat_axis=0, tiled=True)]
    all_to_all x7 -> x0, starting transfers between devices: 33.1 us -> none  [the longest x4 18.1 us: to_all(): return lax.all_to_all(same, axes, split_axis=0, concat_axis=0, tiled=True)]
    reduce_sum x6 -> x0, other arithmetic: 27.6 us -> none  [the longest x1 9.19 us: aligned_device(): jnp.sum(jnp.abs(mg + sg.astype(f32)), axis=1)]
    convert_element_type x2 -> x0, other arithmetic: 12.7 us -> none  [the longest x1 12 us: aligned_device(): narrow_down = (merged_down * (1.0 / scale_down)[:, :, None]).astype(bf16)]
    reshape x2 -> x0, local copies, waits for them, and re-layouts: 9.06 us -> none  [the longest x1 7.69 us: aligned_device(): narrow_down.reshape(experts, zero, width // zero, rows)]
  transfers between devices with their start and end apart: 7 -> 0, of which waited for: 6 -> 0; matrix products, arithmetic and copies ran while one was open for 14% -> 0% of each run, Pallas kernels for 12% -> 0%
where the time goes in v1:
time: 296 us
  Pallas kernels  295 us (100%)
    pallas_call x1, Pallas kernels, fast_device(): pl.pallas_call(functools.partial(exchange_kernel, bank, zero), in_specs=[...  287 us
    pallas_call x1, Pallas kernels, fast_device(): pl.pallas_call(functools.partial(store_kernel, zero), in_specs=[vmem] * 7...  8.65 us

profile of v1, /device:TPU:0, one launch (start us, length us, event | category | flops | bytes accessed | tf_op | source)
XLA Modules:
  0.0 295.8 jit_solution(9112852497083188923)
XLA Ops:
  0.6 286.5 %shard_map.135 = (bf16[16,2048,128]{2,1,0:T(8,128)(2,1)S(1)}, bf16[16,2048,128]{2,1,0:T(8,128)(2,1)S(1)}, bf16[16,8,128,256]{3,2,1,0:T(8,128)(2,1)S(1)}, f32[16,...) custom-call(f32[16,256,1024]{2,1,0:T(8,128)} %refs_0_.1, ...), custom_call_target="tpu_custom_call" | custom-call | tf_op jit(solution)/shard_map/pallas_call | solution.py:362
  287.1 8.7 %shard_map.136 = (bf16[16,2048,128]{2,1,0:T(8,128)(2,1)}, bf16[16,2048,128]{2,1,0:T(8,128)(2,1)}, bf16[16,128,2048]{2,1,0:T(8,128)(2,1)}, f32[16,128]{1,0:T(8,12...) custom-call(bf16[16,2048,128]{2,1,0:T(8,128)(2,1)S(1)} %get-tuple-element.21.refs_0_, ...), custom_call_target="tpu_custom_call" | custom-call | tf_op jit(solution)/shard_map/pallas_call | solution.py:399

commit v2 on v1

--- a/solution.py
+++ b/solution.py
@@ -33,9 +33,9 @@
     (mg, sg, mu, su, md, sd, rw, gain,
      land_gate, land_up, land_down, scale_gate, scale_up, scale_down, router,
      sum_m, sum_s, sum_dm, sum_ds, in_m, in_s, in_dm, in_ds, stage, stage_down,
-     first, first_got, first_inv, part, part_got, total, inverse,
+     first, first_got, first_inv, part, part_got, pair_got, fold, fold_got, total, inverse,
      rw_v, gain_v, router_part,
-     sum_sem, in_sem, stage_sem, data_sem, small_sem, router_sem) = refs
+     sum_sem, in_sem, stage_sem, data_sem, small_sem, fold_sem, router_sem) = refs
     experts, rows, width = mg.shape
     piece = width // zero
     model = rows * zero
@@ -46,6 +46,10 @@
     lands = (land_gate, land_up, land_down)
     scales = (scale_gate, scale_up, scale_down)
     order = send_order(zero)
+    folds = fold_sem.shape[0] // 2 - 2
+    half = width // 2
+    my_half = pl.ds(pl.multiple_of((me % 2) * half, half), half)
+    its_half = pl.ds(pl.multiple_of((1 - me % 2) * half, half), half)
 
     def peer(d):
         return flip(me, d, zero)
@@ -106,7 +110,14 @@
             found.append(jnp.sum(acc.T, axis=0, keepdims=True))
         part[g, pl.ds(j, 1), :] = jnp.concatenate(found, axis=1)
 
-    def sum_experts(g, low, high, last=True):
+    def sum_first():
+        for j in range(FIRST):
+            finish(scale_reads(0, j, j))
+            v = row_sum(in_m.at[j], in_s.at[j])
+            part[0, j : j + 1, :] = v
+            first[j : j + 1, :] = v
+
+    def sum_experts(g, low=0):
         m, base = g // per, (g % per) * GROUP
 
         def body(j, _):
@@ -115,8 +126,6 @@
             if m < 2:
                 v = row_sum(sum_m.at[slot], sum_s.at[slot])
                 part[g, pl.ds(j, 1), :] = v
-                if high == FIRST:
-                    first[pl.ds(j, 1), :] = v
             else:
                 store_column_sums(sum_dm.at[slot], sum_ds.at[slot], g, j)
 
@@ -126,54 +135,79 @@
 
             return 0
 
-        lax.fori_loop(low, high, body, 0)
-        if last and g + 1 < 3 * per:
+        lax.fori_loop(low, GROUP, body, 0)
+        if g + 1 < 3 * per:
             for j in range(AHEAD):
                 start(sum_reads((g + 1) // per, ((g + 1) % per) * GROUP + j, j))
 
-    def scatter_sums(g):
+    def scatter_sums():
         for d in order:
-            send(part.at[g, :, columns(peer(d))], part_got.at[g, d - 1],
-                 small_sem.at[0, g], small_sem.at[1, g], d)
-
-    def gather_totals(g):
-        await_bytes(part_got.at[g], small_sem.at[1, g])
-        t = part[g, :, columns(me)]
+            send(part.at[0, :, columns(peer(d))], part_got.at[d - 1],
+                 small_sem.at[0], small_sem.at[1], d)
+
+    def gather_totals():
+        await_bytes(part_got, small_sem.at[1])
+        t = part[0, :, columns(me)]
         for d in range(1, zero):
-            t = t + part_got[g, d - 1]
-        total[g, :, columns(me)] = t
-        m, base = g // per, (g % per) * GROUP
-        scales[m][base : base + GROUP, :] = t / model
+            t = t + part_got[d - 1]
+        total[0, :, columns(me)] = t
+        scales[0][:GROUP, :] = t / model
         for d in order:
-            mine = total.at[g, :, columns(me)]
-            send(mine, mine, small_sem.at[2, g], small_sem.at[3, g], d)
+            mine = total.at[0, :, columns(me)]
+            send(mine, mine, small_sem.at[2], small_sem.at[3], d)
 
     def take_totals(g):
-        await_bytes(part_got.at[g], small_sem.at[3, g])
+        if g:
+            await_bytes(pair_got.at[g], fold_sem.at[2 * folds + 3, g])
+            m, base = g // per, (g % per) * GROUP
+            scales[m][base : base + GROUP, :] = total[g, :, columns(me)] / model
+        else:
+            await_bytes(part_got, small_sem.at[3])
         for k in range(zero):
             inverse[g, k] = 1.0 / (total[g, :, k * piece : (k + 1) * piece] / model)
 
-
-    def send_expert(m, e, row, slot, fresh=False):
-        finish(scale_reads(m, e, lax.rem(e, READS)))
+    def pair_sums(g):
+        send(part.at[g, :, its_half], pair_got.at[g], fold_sem.at[0, g], fold_sem.at[1, g], 1)
+
+    def fold_sums(g, i):
+        for i in range(i, folds + 1 if i == 2 else min(i, folds) + 1):
+            if i:
+                await_bytes(pair_got.at[g], fold_sem.at[2 * i + 1, g])
+                h = fold[g, i - 1] + fold_got[g, i - 1]
+            else:
+                await_bytes(pair_got.at[g], fold_sem.at[1, g])
+                h = part[g, :, my_half] + pair_got[g]
+            sems = fold_sem.at[2 * i + 2, g], fold_sem.at[2 * i + 3, g]
+            if i < folds:
+                fold[g, i] = h
+                send(fold.at[g, i], fold_got.at[g, i], *sems, 2 << i)
+            else:
+                total[g, :, my_half] = h
+                there = total.at[g, :, my_half]
+                send(there, there, *sems, 1)
+
+
+    def send_expert(m, e, row, slot, fresh=False, ready=False):
+        if not ready:
+            finish(scale_reads(m, e, lax.rem(e, READS)))
         b = lax.rem(e, READS)
         staged = stage if m < 2 else stage_down
         sem = stage_sem.at[int(m == 2), slot]
         if not fresh:
             await_bytes(staged.at[slot], sem)
-        half = rows // 2
+        lot = rows // 2
         for d in order + [0]:
             k = peer(d)
             cut = columns(k)
             scale = row(k)
             if m < 2:
                 for h in range(2):
-                    r = slice(h * half, (h + 1) * half)
+                    r = slice(h * lot, (h + 1) * lot)
                     x = (in_m[b, r, cut] + in_s[b, r, cut].astype(f32)) * scale
                     if d:
                         stage[slot, d - 1, r, :] = x.astype(bf16)
                     else:
-                        at = pl.ds(pl.multiple_of(me * rows + h * half, half), half)
+                        at = pl.ds(pl.multiple_of(me * rows + h * lot, lot), lot)
                         lands[m][e, at, :] = x.astype(bf16)
                 there = lands[m].at[e, pl.ds(pl.multiple_of(me * rows, rows), rows)]
             else:
@@ -216,10 +250,12 @@
             pltpu.make_async_copy(gain, gain_v, router_sem.at[1]),
         )
 
-    def send_router():
+    def fold_router():
         finish(router_reads())
         router_part[...] = (rw_v[...] * gain_v[...]).astype(bf16)
         router[own_experts, own_rows] = router_part[...]
+
+    def send_router():
         for d in order:
             send(router_part, router.at[own_experts, own_rows], router_sem.at[2], router_sem.at[3], d)
 
@@ -240,19 +276,20 @@
         pl.semaphore_signal(
             barrier, inc=1, device_id={"bank": (my_bank + d) % bank}, device_id_type=MESH)
 
-    for j in range(AHEAD):
-        start(sum_reads(0, j, j))
-    for j in range(READS):
+    start(router_reads())
+    for j in range(FIRST):
         start(scale_reads(0, j, j))
-        start(scale_reads(2, j, j))
-    start(router_reads())
-    sum_experts(0, 0, FIRST, last=False)
+    fold_router()
+    for j in range(FIRST, FIRST + AHEAD):
+        start(sum_reads(0, j, j % AHEAD))
+    sum_first()
     pl.semaphore_wait(barrier, zero - 1 + bank - 1)
     for d in order:
-        send(first, first_got.at[d - 1], small_sem.at[4, 0], small_sem.at[4, 1], d)
-    sum_experts(0, FIRST, GROUP)
-    scatter_sums(0)
-    await_bytes(first_got, small_sem.at[4, 1])
+        send(first, first_got.at[d - 1], small_sem.at[4], small_sem.at[5], d)
+    send_router()
+    sum_experts(0, FIRST)
+    scatter_sums()
+    await_bytes(first_got, small_sem.at[5])
     t = first[...]
     for d in range(1, zero):
         t = t + first_got[d - 1]
@@ -260,57 +297,71 @@
         first_inv[k] = 1.0 / (t[:, k * piece : (k + 1) * piece] / model)
 
     def send_first(j):
-        send_expert(0, j, lambda k: first_inv[k, j : j + 1, :], j, fresh=True)
+        send_expert(0, j, lambda k: first_inv[k, j : j + 1, :], j, fresh=True, ready=True)
         start(scale_reads(0, j + READS, j % READS))
 
     send_first(0)
-    sum_experts(1, 0, GROUP)
-    scatter_sums(1)
-    gather_totals(0)
+    sum_experts(1)
+    pair_sums(1)
+    gather_totals()
     send_first(1)
-    send_router()
+    fold_sums(1, 0)
     take_totals(0)
     send_range(0, 2, 4, fresh=True)
-    gather_totals(1)
-    sum_experts(2, 0, GROUP)
-    scatter_sums(2)
+    sum_experts(2)
+    pair_sums(2)
+    fold_sums(1, 1)
+    fold_sums(2, 0)
     send_range(0, 4, 6)
-    sum_experts(3, 0, GROUP)
-    scatter_sums(3)
+    fold_sums(1, 2)
+    fold_sums(2, 1)
+    sum_experts(3)
+    pair_sums(3)
     send_range(0, 6, 7)
-    gather_totals(2)
+    fold_sums(3, 0)
     send_range(0, 7, 8)
     take_totals(1)
     send_range(0, 8, 10)
-    sum_experts(4, 0, GROUP)
-    scatter_sums(4)
-    gather_totals(3)
-    send_range(0, 10, 12)
-    sum_experts(5, 0, GROUP)
-    scatter_sums(5)
+    fold_sums(2, 2)
+    fold_sums(3, 1)
+    sum_experts(4)
+    pair_sums(4)
+    send_range(0, 10, 11)
+    fold_sums(4, 0)
+    send_range(0, 11, 12)
+    fold_sums(3, 2)
+    fold_sums(4, 1)
+    sum_experts(5)
+    pair_sums(5)
+    send_range(0, 12, 13)
+    fold_sums(5, 0)
     share_router()
-    send_range(0, 12, 14)
-    gather_totals(4)
+    send_range(0, 13, 14)
+    fold_sums(4, 2)
+    fold_sums(5, 1)
     send_range(0, 14, 16)
     for j in range(READS):
         start(scale_reads(1, j, j))
-    gather_totals(5)
+        start(scale_reads(2, j, j))
+    fold_sums(5, 2)
     take_totals(2)
     take_totals(3)
-    send_range(1, 0, 4)
+    send_range(1, 0, 2)
     take_totals(4)
     take_totals(5)
-    send_range(1, 4, 16)
+    send_range(1, 2, experts)
     send_range(2, 0, SLOTS, fresh=True)
     send_range(2, SLOTS, experts)
 
     for s in range(SLOTS):
         await_bytes(stage.at[s], stage_sem.at[0, s])
         await_bytes(stage_down.at[s], stage_sem.at[1, s])
-    await_bytes(first_got, small_sem.at[4, 0])
-    for g in range(3 * per):
-        await_bytes(part_got.at[g], small_sem.at[0, g])
-        await_bytes(part_got.at[g], small_sem.at[2, g])
+    await_bytes(first_got, small_sem.at[4])
+    await_bytes(part_got, small_sem.at[0])
+    await_bytes(part_got, small_sem.at[2])
+    for g in range(1, 3 * per):
+        for i in range(folds + 2):
+            await_bytes(pair_got.at[g], fold_sem.at[2 * i, g])
     await_bytes(router.at[pl.ds(0, c), pl.ds(0, (zero - 1) * rows)], router_sem.at[2])
     if bank > 1:
         await_bytes(router.at[pl.ds(0, (bank - 1) * c)], router_sem.at[4])
@@ -347,6 +398,7 @@
     piece = width // zero
     c = router_weight.shape[1]
     groups = 3 * experts // GROUP
+    folds = zero.bit_length() - 2
     anywhere = pl.BlockSpec(memory_space=pl.ANY)
     vmem = pl.BlockSpec(memory_space=pltpu.VMEM)
     shapes = (
@@ -379,7 +431,10 @@
             pltpu.VMEM((zero - 1, FIRST, width), f32),
             pltpu.VMEM((zero, FIRST, piece), f32),
             pltpu.VMEM((groups, GROUP, width), f32),
-            pltpu.VMEM((groups, zero - 1, GROUP, piece), f32),
+            pltpu.VMEM((zero - 1, GROUP, piece), f32),
+            pltpu.VMEM((groups, GROUP, width // 2), f32),
+            pltpu.VMEM((groups, folds, GROUP, width // 2), f32),
+            pltpu.VMEM((groups, folds, GROUP, width // 2), f32),
             pltpu.VMEM((groups, GROUP, width), f32),
             pltpu.VMEM((groups, zero, GROUP, piece), f32),
             pltpu.VMEM((c, rows), f32),
@@ -389,7 +444,8 @@
             dma((2, 2, READS)),
             dma((2, SLOTS)),
             dma((3, zero - 1)),
-            dma((5, groups)),
+            dma((6,)),
+            dma((2 * folds + 4, groups)),
             dma((6,)),
         ],
         compiler_params=pltpu.CompilerParams(
@@ -437,7 +493,7 @@
     zero = sizes[1]
     experts, rows, width = mg.shape
     c = router_weight.shape[1]
-    if zero < 2 or zero & (zero - 1) or experts != 2 * GROUP or experts % zero:
+    if zero < 4 or zero & (zero - 1) or experts != 2 * GROUP or experts % zero:
         return False
     if width % zero or (width // zero) % 128 or rows % 256 or c % 16:
         return False

time: 296 us -> 293 us (0.990)
  no operation moved by 1% of the time
where the time goes in v2:
time: 293 us
  Pallas kernels  293 us (100%)
    pallas_call x1, Pallas kernels, fast_device(): pl.pallas_call(functools.partial(exchange_kernel, bank, zero), in_specs=[...  284 us
    pallas_call x1, Pallas kernels, fast_device(): pl.pallas_call(functools.partial(store_kernel, zero), in_specs=[vmem] * 7...  8.65 us

profile of v2, /device:TPU:0, one launch (start us, length us, event | category | flops | bytes accessed | tf_op | source)
XLA Modules:
  0.0 293.2 jit_solution(3486042509962157087)
XLA Ops:
  0.6 283.9 %shard_map.135 = (bf16[16,2048,128]{2,1,0:T(8,128)(2,1)S(1)}, bf16[16,2048,128]{2,1,0:T(8,128)(2,1)S(1)}, bf16[16,8,128,256]{3,2,1,0:T(8,128)(2,1)S(1)}, f32[16,...) custom-call(f32[16,256,1024]{2,1,0:T(8,128)} %refs_0_.1, ...), custom_call_target="tpu_custom_call" | custom-call | tf_op jit(solution)/shard_map/pallas_call | solution.py:414
  284.5 8.7 %shard_map.136 = (bf16[16,2048,128]{2,1,0:T(8,128)(2,1)}, bf16[16,2048,128]{2,1,0:T(8,128)(2,1)}, bf16[16,128,2048]{2,1,0:T(8,128)(2,1)}, f32[16,128]{1,0:T(8,12...) custom-call(bf16[16,2048,128]{2,1,0:T(8,128)(2,1)S(1)} %get-tuple-element.21.refs_0_, ...), custom_call_target="tpu_custom_call" | custom-call | tf_op jit(solution)/shard_map/pallas_call | solution.py:455

commit v3 on v2

--- a/solution.py
+++ b/solution.py
@@ -14,6 +14,8 @@
 AHEAD = 4
 READS = 2
 SLOTS = 4
+LATE = 10
+LAST = 1
 
 
 def flip(index, bits, size):
@@ -25,21 +27,26 @@
     return out
 
 
+def even(zero):
+    return range(zero - 2, 0, -2)
+
+
 def send_order(zero):
     return sorted(range(1, zero), key=lambda d: (d == 1, d & 1, -d))
 
 
 def exchange_kernel(bank, zero, *refs):
     (mg, sg, mu, su, md, sd, rw, gain,
-     land_gate, land_up, land_down, scale_gate, scale_up, scale_down, router,
+     land_gate, land_up, land_down, scale_gate, scale_up, scale_down, router, held,
      sum_m, sum_s, sum_dm, sum_ds, in_m, in_s, in_dm, in_ds, stage, stage_down,
      first, first_got, first_inv, part, part_got, pair_got, fold, fold_got, total, inverse,
      rw_v, gain_v, router_part,
-     sum_sem, in_sem, stage_sem, data_sem, small_sem, fold_sem, router_sem) = refs
+     sum_sem, in_sem, stage_sem, data_sem, small_sem, fold_sem, late_sem, router_sem) = refs
     experts, rows, width = mg.shape
     piece = width // zero
     model = rows * zero
     per = experts // GROUP
+    early = experts - held.shape[0]
     me = lax.axis_index("zero")
     my_bank = lax.axis_index("bank")
     masters, seconds = (mg, mu, md), (sg, su, sd)
@@ -115,7 +122,12 @@
             finish(scale_reads(0, j, j))
             v = row_sum(in_m.at[j], in_s.at[j])
             part[0, j : j + 1, :] = v
-            first[j : j + 1, :] = v
+            first[j] = v
+            if j == 0:
+                pl.semaphore_wait(barrier, zero - 1 + bank - 1)
+            for d in order:
+                send(first.at[j], first_got.at[j, d - 1],
+                     small_sem.at[4 + 2 * j], small_sem.at[5 + 2 * j], d)
 
     def sum_experts(g, low=0):
         m, base = g // per, (g % per) * GROUP
@@ -187,14 +199,14 @@
                 send(there, there, *sems, 1)
 
 
-    def send_expert(m, e, row, slot, fresh=False, ready=False):
+    def send_expert(m, e, row, slot, before=0, hold=False, ready=False):
         if not ready:
             finish(scale_reads(m, e, lax.rem(e, READS)))
         b = lax.rem(e, READS)
         staged = stage if m < 2 else stage_down
         sem = stage_sem.at[int(m == 2), slot]
-        if not fresh:
-            await_bytes(staged.at[slot], sem)
+        if before:
+            await_bytes(staged.at[slot, pl.ds(0, before)], sem)
         lot = rows // 2
         for d in order + [0]:
             k = peer(d)
@@ -215,21 +227,23 @@
                 for c in range(rows // 128):
                     r = slice(c * 128, (c + 1) * 128)
                     x = (in_dm[b, cut, r] + in_ds[b, cut, r].astype(f32)) * t
-                    if d:
+                    if d and hold and d % 2 == 0:
+                        held[e - early, d // 2 - 1, :, r] = x.astype(bf16)
+                    elif d:
                         stage_down[slot, d - 1, :, r] = x.astype(bf16)
                     else:
                         land_down[e, me, :, r] = x.astype(bf16)
                 there = land_down.at[e, me]
-            if d:
+            if d and not (hold and d % 2 == 0):
                 send(staged.at[slot, d - 1], there, sem, data_sem.at[m, d - 1], d)
 
     def scaled_row(g, j):
         return lambda k: inverse[g, k, pl.ds(j, 1), :]
 
-    def send_range(m, low, high, fresh=False):
+    def send_range(m, low, high, before=zero - 1, hold=False):
         def body(e, _):
             send_expert(m, e, scaled_row(m * per + e // GROUP, lax.rem(e, GROUP)),
-                        lax.rem(e, SLOTS), fresh)
+                        lax.rem(e, SLOTS), before, hold)
 
             @pl.when(e + READS < experts)
             def _():
@@ -283,21 +297,17 @@
     for j in range(FIRST, FIRST + AHEAD):
         start(sum_reads(0, j, j % AHEAD))
     sum_first()
-    pl.semaphore_wait(barrier, zero - 1 + bank - 1)
-    for d in order:
-        send(first, first_got.at[d - 1], small_sem.at[4], small_sem.at[5], d)
     send_router()
     sum_experts(0, FIRST)
     scatter_sums()
-    await_bytes(first_got, small_sem.at[5])
-    t = first[...]
-    for d in range(1, zero):
-        t = t + first_got[d - 1]
-    for k in range(zero):
-        first_inv[k] = 1.0 / (t[:, k * piece : (k + 1) * piece] / model)
-
     def send_first(j):
-        send_expert(0, j, lambda k: first_inv[k, j : j + 1, :], j, fresh=True, ready=True)
+        await_bytes(first_got.at[j], small_sem.at[5 + 2 * j])
+        t = first[j]
+        for d in range(1, zero):
+            t = t + first_got[j, d - 1]
+        for k in range(zero):
+            first_inv[j, k] = 1.0 / (t[:, k * piece : (k + 1) * piece] / model)
+        send_expert(0, j, lambda k: first_inv[j, k], j, ready=True)
         start(scale_reads(0, j + READS, j % READS))
 
     send_first(0)
@@ -307,7 +317,7 @@
     send_first(1)
     fold_sums(1, 0)
     take_totals(0)
-    send_range(0, 2, 4, fresh=True)
+    send_range(0, 2, 4, before=0)
     sum_experts(2)
     pair_sums(2)
     fold_sums(1, 1)
@@ -350,13 +360,26 @@
     take_totals(4)
     take_totals(5)
     send_range(1, 2, experts)
-    send_range(2, 0, SLOTS, fresh=True)
-    send_range(2, SLOTS, experts)
+    send_range(2, 0, SLOTS, before=0)
+    send_range(2, SLOTS, early)
+    send_range(2, early, early + SLOTS, hold=True)
+    send_range(2, early + SLOTS, experts, before=zero // 2, hold=True)
+
+    @pl.when(me % 2 != LAST)
+    def _():
+        def body(e, _):
+            for d in even(zero):
+                send(held.at[e, d // 2 - 1], land_down.at[early + e, me],
+                     late_sem.at[0], late_sem.at[1], d)
+            return 0
+
+        lax.fori_loop(0, experts - early, body, 0)
 
     for s in range(SLOTS):
         await_bytes(stage.at[s], stage_sem.at[0, s])
-        await_bytes(stage_down.at[s], stage_sem.at[1, s])
-    await_bytes(first_got, small_sem.at[4])
+        await_bytes(stage_down.at[s, pl.ds(0, zero // 2)], stage_sem.at[1, s])
+    for j in range(FIRST):
+        await_bytes(first_got.at[j], small_sem.at[4 + 2 * j])
     await_bytes(part_got, small_sem.at[0])
     await_bytes(part_got, small_sem.at[2])
     for g in range(1, 3 * per):
@@ -369,13 +392,63 @@
     for d in range(1, zero):
         await_bytes(land_gate.at[:, pl.ds(0, rows)], data_sem.at[0, d - 1])
         await_bytes(land_up.at[:, pl.ds(0, rows)], data_sem.at[1, d - 1])
-        await_bytes(land_down.at[:, 0], data_sem.at[2, d - 1])
+        await_bytes(land_down.at[pl.ds(0, experts if d % 2 else early), 0], data_sem.at[2, d - 1])
+
+    @pl.when(me % 2 != LAST)
+    def _():
+        await_bytes(held, late_sem.at[0])
+        await_bytes(held, late_sem.at[1])
+
+
+def late_kernel(zero, held, stored, late, late_sem):
+    me = lax.axis_index("zero")
+
+    @pl.when(me % 2 == LAST)
+    def _():
+        barrier = pltpu.get_barrier_semaphore()
+        for d in even(zero):
+            pl.semaphore_signal(
+                barrier, inc=1, device_id={"zero": flip(me, d, zero)}, device_id_type=MESH)
+        pl.semaphore_wait(barrier, zero // 2 - 1)
+
+        def body(e, _):
+            for d in even(zero):
+                pltpu.make_async_remote_copy(
+                    src_ref=held.at[e, d // 2 - 1], dst_ref=late.at[e, d // 2 - 1],
+                    send_sem=late_sem.at[0], recv_sem=late_sem.at[1],
+                    device_id={"zero": flip(me, d, zero)}, device_id_type=MESH,
+                ).start()
+            return 0
+
+        lax.fori_loop(0, held.shape[0], body, 0)
+        for i in range(2):
+            pltpu.make_async_copy(held, held, late_sem.at[i]).wait()
+
+
+def place_kernel(zero, down, late, out, sem):
+    me = lax.axis_index("zero")
+    count, _, piece, rows = late.shape
+    experts = out.shape[0]
+
+    @pl.when(me % 2 == LAST)
+    def _():
+        copies = []
+        for d in even(zero):
+            at = pl.ds(pl.multiple_of(flip(me, d, zero) * rows, rows), rows)
+            copies.append(pltpu.make_async_copy(
+                late.at[:, d // 2 - 1], out.at[pl.ds(experts - count, count), :, at],
+                sem.at[d // 2 - 1]))
+        for c in copies:
+            c.start()
+        for c in copies:
+            c.wait()
 
 
 def store_kernel(zero, *refs):
     gate, up, down, *small = refs[:7]
     out_gate, out_up, out_down, *small_out = refs[7:14]
-    sem = refs[14]
+    token, sem = refs[14:]
+    token[...] = jnp.zeros_like(token)
     rows = down.shape[3]
     copies = []
     for src, dst in ((gate, out_gate), (up, out_up)):
@@ -409,12 +482,13 @@
         ((experts, piece), f32),
         ((experts, piece), f32),
         ((bank * c, zero * rows), bf16),
+        ((experts * LATE // 16, zero // 2 - 1, piece, rows), bf16),
     )
     dma = pltpu.SemaphoreType.DMA
-    landed = pl.pallas_call(
+    *landed, held = pl.pallas_call(
         functools.partial(exchange_kernel, bank, zero),
         in_specs=[anywhere] * 8,
-        out_specs=[vmem] * 7,
+        out_specs=[vmem] * 8,
         out_shape=[pltpu.VMEM(*s) for s in shapes],
         scratch_shapes=[
             pltpu.VMEM((AHEAD, rows, width), f32),
@@ -427,9 +501,9 @@
             pltpu.VMEM((READS, width, rows), bf16),
             pltpu.VMEM((SLOTS, zero - 1, rows, piece), bf16),
             pltpu.VMEM((SLOTS, zero - 1, piece, rows), bf16),
-            pltpu.VMEM((FIRST, width), f32),
-            pltpu.VMEM((zero - 1, FIRST, width), f32),
-            pltpu.VMEM((zero, FIRST, piece), f32),
+            pltpu.VMEM((FIRST, 1, width), f32),
+            pltpu.VMEM((FIRST, zero - 1, 1, width), f32),
+            pltpu.VMEM((FIRST, zero, 1, piece), f32),
             pltpu.VMEM((groups, GROUP, width), f32),
             pltpu.VMEM((zero - 1, GROUP, piece), f32),
             pltpu.VMEM((groups, GROUP, width // 2), f32),
@@ -444,23 +518,44 @@
             dma((2, 2, READS)),
             dma((2, SLOTS)),
             dma((3, zero - 1)),
-            dma((6,)),
+            dma((4 + 2 * FIRST,)),
             dma((2 * folds + 4, groups)),
+            dma((2,)),
             dma((6,)),
         ],
         compiler_params=pltpu.CompilerParams(
             collective_id=0, has_side_effects=True, vmem_limit_bytes=34 << 20),
     )(mg, sg, mu, su, md, sd, router_weight.T, router_gain.reshape(1, -1))
-    outs = shapes[:2] + (((experts, piece, zero * rows), bf16),) + shapes[3:]
-    *stored, router = pl.pallas_call(
+    token = ((8, 128), f32)
+    outs = shapes[:2] + (((experts, piece, zero * rows), bf16),) + shapes[3:7]
+    *stored, router, token = pl.pallas_call(
         functools.partial(store_kernel, zero),
         in_specs=[vmem] * 7,
-        out_specs=[anywhere] * 7,
-        out_shape=[jax.ShapeDtypeStruct(*s) for s in outs],
+        out_specs=[anywhere] * 7 + [vmem],
+        out_shape=[jax.ShapeDtypeStruct(*s) for s in outs] + [pltpu.VMEM(*token)],
         scratch_shapes=[dma((3 * zero + 4,))],
         compiler_params=pltpu.CompilerParams(vmem_limit_bytes=1 << 20),
     )(*landed)
-    return (*stored, router.T)
+    gate, up, down, *scales = stored
+    late = pl.pallas_call(
+        functools.partial(late_kernel, zero),
+        in_specs=[vmem, vmem],
+        out_specs=vmem,
+        out_shape=pltpu.VMEM(*shapes[7]),
+        scratch_shapes=[dma((2,))],
+        compiler_params=pltpu.CompilerParams(
+            collective_id=1, has_side_effects=True, vmem_limit_bytes=1 << 20),
+    )(held, token)
+    down = pl.pallas_call(
+        functools.partial(place_kernel, zero),
+        in_specs=[anywhere, vmem],
+        out_specs=anywhere,
+        out_shape=jax.ShapeDtypeStruct(*outs[2]),
+        input_output_aliases={0: 0},
+        scratch_shapes=[dma((zero // 2 - 1,))],
+        compiler_params=pltpu.CompilerParams(vmem_limit_bytes=1 << 20),
+    )(down, late)
+    return (gate, up, down, *scales, router.T)
 
 
 def mine(scale, zero):

time: 293 us -> 284 us (0.969); the launches traced: 293 us -> 280 us
  Pallas kernels: 293 us -> 280 us
    pallas_call x1, Pallas kernels: 284 us -> 271 us  [fast_device(): pl.pallas_call(functools.partial(exchange_kernel, bank, zero), in_specs=[...]
where the time goes in v3:
time: 284 us; the launch traced here: 280 us
  Pallas kernels  280 us (99%)
    pallas_call x1, Pallas kernels, fast_device(): pl.pallas_call(functools.partial(exchange_kernel, bank, zero), in_specs=[...  271 us
    pallas_call x1, Pallas kernels, fast_device(): pl.pallas_call(functools.partial(store_kernel, zero), in_specs=[vmem] * 7...  8.65 us

profile of v3, /device:TPU:0, one launch (start us, length us, event | category | flops | bytes accessed | tf_op | source)
XLA Modules:
  0.0 280.3 jit_solution(3042197830895713537)
XLA Ops:
  0.6 270.9 %shard_map.135 = (bf16[16,2048,128]{2,1,0:T(8,128)(2,1)S(1)}, bf16[16,2048,128]{2,1,0:T(8,128)(2,1)S(1)}, bf16[16,8,128,256]{3,2,1,0:T(8,128)(2,1)S(1)}, f32[16,...) custom-call(f32[16,256,1024]{2,1,0:T(8,128)} %refs_0_.1, ...), custom_call_target="tpu_custom_call" | custom-call | tf_op jit(solution)/shard_map/pallas_call | solution.py:488
  271.6 8.7 %shard_map.136 = (bf16[16,2048,128]{2,1,0:T(8,128)(2,1)}, bf16[16,2048,128]{2,1,0:T(8,128)(2,1)}, bf16[16,128,2048]{2,1,0:T(8,128)(2,1)}, f32[16,128]{1,0:T(8,12...) custom-call(bf16[16,2048,128]{2,1,0:T(8,128)(2,1)S(1)} %get-tuple-element.23.refs_0, ...), custom_call_target="tpu_custom_call" | custom-call | tf_op jit(solution)/shard_map/pallas_call | solution.py:531
  280.3 0.1 shard_map.138
  (1 shorter events, 0.0 us)

commit v4 on v3

--- a/solution.py
+++ b/solution.py
@@ -120,6 +120,9 @@
     def sum_first():
         for j in range(FIRST):
             finish(scale_reads(0, j, j))
+            if j == 0:
+                for i in range(FIRST, FIRST + AHEAD):
+                    start(sum_reads(0, i, i % AHEAD))
             v = row_sum(in_m.at[j], in_s.at[j])
             part[0, j : j + 1, :] = v
             first[j] = v
@@ -294,8 +297,6 @@
     for j in range(FIRST):
         start(scale_reads(0, j, j))
     fold_router()
-    for j in range(FIRST, FIRST + AHEAD):
-        start(sum_reads(0, j, j % AHEAD))
     sum_first()
     send_router()
     sum_experts(0, FIRST)
@@ -338,28 +339,28 @@
     pair_sums(4)
     send_range(0, 10, 11)
     fold_sums(4, 0)
-    send_range(0, 11, 12)
+    send_range(0, 11, 13)
+    sum_experts(5)
+    pair_sums(5)
     fold_sums(3, 2)
     fold_sums(4, 1)
-    sum_experts(5)
-    pair_sums(5)
-    send_range(0, 12, 13)
+    send_range(0, 13, 14)
     fold_sums(5, 0)
     share_router()
-    send_range(0, 13, 14)
-    fold_sums(4, 2)
-    fold_sums(5, 1)
     send_range(0, 14, 16)
     for j in range(READS):
         start(scale_reads(1, j, j))
         start(scale_reads(2, j, j))
-    fold_sums(5, 2)
+    fold_sums(4, 2)
+    fold_sums(5, 1)
     take_totals(2)
     take_totals(3)
     send_range(1, 0, 2)
+    fold_sums(5, 2)
+    send_range(1, 2, 4)
     take_totals(4)
     take_totals(5)
-    send_range(1, 2, experts)
+    send_range(1, 4, experts)
     send_range(2, 0, SLOTS, before=0)
     send_range(2, SLOTS, early)
     send_range(2, early, early + SLOTS, hold=True)

time: 284 us -> 284 us (level)
  no operation moved by 1% of the time
where the time goes in v4:
time: 284 us; the launch traced here: 280 us
  Pallas kernels  280 us (99%)
    pallas_call x1, Pallas kernels, fast_device(): pl.pallas_call(functools.partial(exchange_kernel, bank, zero), in_specs=[...  271 us
    pallas_call x1, Pallas kernels, fast_device(): pl.pallas_call(functools.partial(store_kernel, zero), in_specs=[vmem] * 7...  8.65 us

profile of v4, /device:TPU:0, one launch (start us, length us, event | category | flops | bytes accessed | tf_op | source)
XLA Modules:
  0.0 280.3 jit_solution(14697319721112550680)
XLA Ops:
  0.6 270.9 %shard_map.135 = (bf16[16,2048,128]{2,1,0:T(8,128)(2,1)S(1)}, bf16[16,2048,128]{2,1,0:T(8,128)(2,1)S(1)}, bf16[16,8,128,256]{3,2,1,0:T(8,128)(2,1)S(1)}, f32[16,...) custom-call(f32[16,256,1024]{2,1,0:T(8,128)} %refs_0_.1, ...), custom_call_target="tpu_custom_call" | custom-call | tf_op jit(solution)/shard_map/pallas_call | solution.py:489
  271.6 8.7 %shard_map.136 = (bf16[16,2048,128]{2,1,0:T(8,128)(2,1)}, bf16[16,2048,128]{2,1,0:T(8,128)(2,1)}, bf16[16,128,2048]{2,1,0:T(8,128)(2,1)}, f32[16,128]{1,0:T(8,12...) custom-call(bf16[16,2048,128]{2,1,0:T(8,128)(2,1)S(1)} %get-tuple-element.23.refs_0, ...), custom_call_target="tpu_custom_call" | custom-call | tf_op jit(solution)/shard_map/pallas_call | solution.py:532
  280.3 0.1 shard_map.138
  (1 shorter events, 0.0 us)
